TPU v7x, 32 devices: a whole 2x2x4 slice. The times are simulated.
32 devices in a mesh: tm: 8 (over z, x), env: 4 (over y, core).
Axes of the slice: x: 2, y: 2, z: 4, core: 2. Of those that a mesh axis runs over, the one named last changes fastest.
Arguments:
- init_state: float32 [70, 1024], P(None, 'env'), may hold values from -6 to 6
- torque: float32 [32, 35, 1024], P('tm', None, 'env'), may hold values from -192 to 192
- contact: int32 [32, 1024], P('tm', 'env'), may hold values 0 or 1
- mass_inverse: float32 [16, 35, 35], P('tm'), may hold values from -0.014 to 1.5, as said below
- stiffness: float32 [35], replicated, may hold values from 10 to 100
- damping: float32 [35], replicated, may hold values from 0.5 to 5
- gravity: float32 [35], replicated, may hold values from 1 to 10
- contact_stiffness: float32 [35], replicated, may hold values from 20 to 100
- contact_damping: float32 [35], replicated, may hold values from 0.5 to 3
Outputs:
- final_states: float32 [16, 70, 1024], P('tm', None, 'env')
- corrections: float32 [3, 1024], P(None, 'env')
Inputs may be any that keep to these rules, and one draw needn't show every extreme that they name: `mass_inverse`: each matrix is symmetric, and each diagonal entry exceeds the sum of the magnitudes of the other entries of its row.
All inputs are finite; a program needn't handle non-finite values. No bound on the sum of `contact` on one device may be relied on, other than what follows from the above.
Results may differ from a plain program's by a relative error of at most 0.00025.
Values sent between devices are 32-bit elements; how exact they have to be, the bound alone decides.
A program may use at most 64 MiB of HBM per device.

v0:
```python
import jax
import jax.numpy as jnp
from jax import lax
from jax.sharding import PartitionSpec as P

DOF = 35
HS = 2
SUB = 32
ITERS = 3
step_length = 0.05


def exact_dot(left, right):
    return jnp.dot(left, right, precision=lax.Precision.HIGHEST, preferred_element_type=jnp.float32)


def coarse_one(state_now, torque_steps, mean_steps, inverse, params):
    stiffness, damping, gravity, contact_stiffness, contact_damping = params
    joint_pos = state_now[:DOF]
    joint_vel = state_now[DOF:]
    for step_pos in range(HS):
        spring = (stiffness + gravity + mean_steps[step_pos] * contact_stiffness)[:, None]
        friction = (damping + mean_steps[step_pos] * contact_damping)[:, None]
        force = torque_steps[step_pos] - spring * joint_pos - friction * joint_vel
        joint_vel = joint_vel + step_length * exact_dot(inverse, force)
        joint_pos = joint_pos + step_length * joint_vel
    return jnp.concatenate([joint_pos, joint_vel], axis=0)


def fine_one(state_now, torque_steps, contact_steps, inverse, params):
    stiffness, damping, gravity, contact_stiffness, contact_damping = params
    fine_dt = step_length / SUB
    joint_pair = (state_now[:DOF], state_now[DOF:])
    for step_pos in range(HS):
        torque_here = torque_steps[step_pos]
        contact_here = contact_steps[step_pos][None, :]

        def substep(counter, pair_now):
            joint_pos, joint_vel = pair_now
            force = (
                torque_here
                - stiffness[:, None] * joint_pos
                - damping[:, None] * joint_vel
                - gravity[:, None] * jnp.sin(joint_pos)
                - contact_here
                * (contact_stiffness[:, None] * joint_pos + contact_damping[:, None] * joint_vel)
            )
            joint_vel = joint_vel + fine_dt * exact_dot(inverse, force)
            joint_pos = joint_pos + fine_dt * joint_vel
            return (joint_pos, joint_vel)

        joint_pair = lax.fori_loop(0, SUB, substep, joint_pair, unroll=min(8, SUB))
    return jnp.concatenate([joint_pair[0], joint_pair[1]], axis=0)


def body(
    init_state,
    torque,
    contact,
    mass_inverse,
    stiffness,
    damping,
    gravity,
    contact_stiffness,
    contact_damping,
):
    params = (stiffness, damping, gravity, contact_stiffness, contact_damping)
    local_slices = mass_inverse.shape[0]
    env_local = init_state.shape[1]
    state_rows = init_state.shape[0]
    torque_steps = torque.reshape(local_slices, HS, DOF, env_local)
    contact_float = contact.astype(jnp.float32)
    contact_steps = contact_float.reshape(local_slices, HS, env_local)
    totals = lax.psum(jnp.sum(contact_float, axis=1), "env")
    mean_steps = (totals / (env_local * lax.axis_size("env"))).reshape(local_slices, HS)
    eye_state = jnp.eye(state_rows, dtype=jnp.float32)
    zero_shift = jnp.zeros((state_rows, env_local), jnp.float32)
    no_force = jnp.zeros((local_slices, HS, DOF, 1), jnp.float32)
    step_maps = jax.vmap(coarse_one, in_axes=(None, 0, 0, 0, None))(
        eye_state, no_force, mean_steps, mass_inverse, params
    )
    coarse_free = jax.vmap(coarse_one, in_axes=(0, 0, 0, 0, None))(
        jnp.zeros((local_slices, state_rows, env_local), jnp.float32),
        torque_steps,
        mean_steps,
        mass_inverse,
        params,
    )
    device_map = eye_state
    for slot_pos in range(local_slices):
        device_map = exact_dot(step_maps[slot_pos], device_map)
    all_maps = lax.all_gather(device_map[None], "tm", axis=0, tiled=True)
    my_index = lax.axis_index("tm")

    def backward(product, inputs):
        position, this_map = inputs
        active = position < my_index
        emitted = jnp.where(active, product, 0.0)
        following = jnp.where(active, exact_dot(product, this_map), eye_state)
        return (following, emitted)

    positions = jnp.arange(lax.axis_size("tm"), dtype=jnp.int32)
    lead_map, phi_rows = lax.scan(backward, eye_state, (positions, all_maps), reverse=True)
    lead_state = exact_dot(lead_map, init_state)

    def sweep(offsets):
        local_shift = zero_shift
        for slot_pos in range(local_slices):
            local_shift = exact_dot(step_maps[slot_pos], local_shift) + offsets[slot_pos]
        entry = lead_state + jnp.einsum(
            "mij,mje->ie",
            phi_rows,
            lax.all_gather(local_shift[None], "tm", axis=0, tiled=True),
            precision=lax.Precision.HIGHEST,
        )
        start_list = []
        end_list = []
        current = entry
        for slot_pos in range(local_slices):
            start_list.append(current)
            current = exact_dot(step_maps[slot_pos], current) + offsets[slot_pos]
            end_list.append(current)
        return (jnp.stack(start_list), jnp.stack(end_list))

    starts, ends = sweep(coarse_free)
    fine_all = jax.vmap(fine_one, in_axes=(0, 0, 0, 0, None))
    records = []
    for iteration in range(ITERS):
        fine_end = fine_all(starts, torque_steps, contact_steps, mass_inverse, params)
        jumps = fine_end - jnp.einsum(
            "sij,sje->sie", step_maps, starts, precision=lax.Precision.HIGHEST
        )
        new_starts, new_ends = sweep(jumps)
        local_max = jnp.max(jnp.sqrt(jnp.sum((new_ends - ends) ** 2, axis=1)), axis=0)
        records.append(lax.pmax(local_max, "tm"))
        starts, ends = (new_starts, new_ends)
    corrections = jnp.stack(records)
    return (ends, corrections)


def solution(mesh):
    placed = (
        P(None, "env"),
        P("tm", None, "env"),
        P("tm", "env"),
        P("tm", None, None),
        P(),
        P(),
        P(),
        P(),
        P(),
    )
    return jax.shard_map(
        body,
        mesh=mesh,
        in_specs=placed,
        out_specs=(P("tm", None, "env"), P(None, "env")),
        check_vma=False,
    )
```

profile of v0, /device:TPU:0, one launch (start us, length us, event | category | flops | bytes accessed | tf_op | source)
XLA Modules:
  0.0 318.0 jit_solution(16330962543061578949)
XLA Ops:
  0.6 0.8 convert_reduce_fusion
  1.5 8.4 %psum.7 = f32[4]{0:T(128)S(1)} all-reduce(f32[4]{0:T(128)S(1)} %convert_reduce_fusion), channel_id=1, replica_groups=mesh['tm'=8,'env'=4] {'env'}, use_global_device_ids=true, to_apply=%region_1.0 | all-reduce | flops 4 | bytes 32 | tf_op jit(solution)/shard_map/psum | solution.py:74
  10.2 0.6 copy-done.4
  10.8 0.6 copy-done.1
  11.8 0.7 copy-done.6
  13.6 31.3 %all-gather.5 = f32[8,70,70]{2,1,0:T(8,128)S(1)} all-gather(f32[1,70,70]{2,1,0:T(8,128)S(1)} %convolution_bitcast_fusion.5), channel_id=2, replica_groups=mesh['tm'=8,'env'=4] {'tm'}, dimensions={0}, use_global_device_ids=true | all-gather | bytes 176400 | tf_op jit(solution)/shard_map/all_gather | solution.py:92
  44.9 12.7 %while.95 = (s32[]{:T(128)}, f32[70,70]{0,1:T(8,128)S(1)}, f32[8,70,70]{1,2,0:T(8,128)S(1)}, s32[8]{0:T(128)S(1)}, s32[]{:T(128)}, /*index=5*/f32[8,70,70]{2,1,0:T(8,128)S(1)}, s32[]{:T(128)}, s32[]{:T(128)}) while((s32[]{:T(128)}, f32[70,70]{0,1:T(8,128)S(1)}, f32[8,70,70]{1,2,0:T(8,128)S(1)}, s32[8]{0:T(128)S(1)}, s32[]{:T(128)}, ...), condition=%wide.region_3.4_spmd.clone, body=%wide.region_2.3_spmd.clone.sunk | while | flops 4135604 | bytes 206392 | solution.py:103
  44.9 0.6 dynamic_slice.29
  46.5 0.6 dynamic_slice.29
  48.1 0.6 dynamic_slice.29
  49.7 0.6 dynamic_slice.29
  51.2 0.6 dynamic_slice.29
  52.8 0.6 dynamic_slice.29
  54.4 0.6 dynamic_slice.29
  56.0 0.6 dynamic_slice.29
  59.6 31.5 %all-gather.6 = f32[8,70,256]{2,1,0:T(8,128)S(1)} all-gather(f32[1,70,256]{2,1,0:T(8,128)S(1)} %fusion.1027), channel_id=3, replica_groups=mesh['tm'=8,'env'=4] {'tm'}, dimensions={0}, use_global_device_ids=true | all-gather | bytes 645120 | tf_op jit(solution)/shard_map/all_gather | solution.py:113
  91.1 0.7 fusion.1026
  92.3 0.7 copy-done.8
  93.1 17.1 %while.89 = (s32[]{:T(128)}, f32[2,35,256]{2,1,0:T(8,128)S(1)}, f32[2,35,256]{2,1,0:T(8,128)S(1)}, f32[35]{0:T(128)S(1)}, f32[2,35,256]{2,1,0:T(8,128)S(1)}, /*i...) while((s32[]{:T(128)}, f32[2,35,256]{2,1,0:T(8,128)S(1)}, ...), condition=%wide.region_5.6_spmd, body=%wide.region_4.5_spmd.sunk | while | flops 62504960 | bytes 2680981 | solution.py:52
  93.6 0.5 multiply_add_fusion.107
  96.8 0.5 multiply_add_fusion.110
  97.9 0.5 multiply_add_fusion.107
  110.2 17.2 %while.90 = (s32[]{:T(128)}, f32[2,35,256]{2,1,0:T(8,128)S(1)}, f32[2,35,256]{2,1,0:T(8,128)S(1)}, f32[35]{0:T(128)S(1)}, f32[2,35,256]{2,1,0:T(8,128)S(1)}, /*i...) while((s32[]{:T(128)}, f32[2,35,256]{2,1,0:T(8,128)S(1)}, ...), condition=%wide.region_7.8_spmd, body=%wide.region_6.7_spmd.sunk | while | flops 62504960 | bytes 2680981 | solution.py:52
  110.8 0.5 multiply_add_fusion.111
  111.8 0.5 multiply_add_fusion.112
  114.0 0.5 multiply_add_fusion.114
  115.1 0.5 multiply_add_fusion.111
  116.1 0.5 multiply_add_fusion.112
  119.4 0.5 multiply_add_fusion.111
  120.4 0.5 multiply_add_fusion.112
  122.6 0.5 multiply_add_fusion.114
  123.6 0.5 multiply_add_fusion.111
  124.7 0.5 multiply_add_fusion.112
  126.9 0.5 multiply_add_fusion.114
  127.9 31.5 %all-gather.7 = f32[8,70,256]{2,1,0:T(8,128)S(1)} all-gather(f32[1,70,256]{2,1,0:T(8,128)S(1)} %fusion.1025), channel_id=4, replica_groups=mesh['tm'=8,'env'=4] {'tm'}, dimensions={0}, use_global_device_ids=true | all-gather | bytes 645120 | tf_op jit(solution)/shard_map/all_gather | solution.py:113
  159.4 0.7 fusion.1024
  160.5 17.2 %while.91 = (s32[]{:T(128)}, f32[2,35,256]{2,1,0:T(8,128)S(1)}, f32[2,35,256]{2,1,0:T(8,128)S(1)}, f32[35]{0:T(128)S(1)}, f32[2,35,256]{2,1,0:T(8,128)S(1)}, /*i...) while((s32[]{:T(128)}, f32[2,35,256]{2,1,0:T(8,128)S(1)}, ...), condition=%wide.region_9.10_spmd, body=%wide.region_8.9_spmd.sunk | while | flops 62504960 | bytes 2680981 | solution.py:52
  177.7 17.2 %while.92 = (s32[]{:T(128)}, f32[2,35,256]{2,1,0:T(8,128)S(1)}, f32[2,35,256]{2,1,0:T(8,128)S(1)}, f32[35]{0:T(128)S(1)}, f32[2,35,256]{2,1,0:T(8,128)S(1)}, /*i...) while((s32[]{:T(128)}, f32[2,35,256]{2,1,0:T(8,128)S(1)}, ...), condition=%wide.region_11.12_spmd, body=%wide.region_10.11_spmd.sunk | while | flops 62504960 | bytes 2680981 | solution.py:52
  178.2 0.5 multiply_add_fusion.119
  179.3 0.5 multiply_add_fusion.120
  182.5 0.5 multiply_add_fusion.119
  183.6 0.5 multiply_add_fusion.120
  186.8 0.5 multiply_add_fusion.119
  187.9 0.5 multiply_add_fusion.120
  191.1 0.5 multiply_add_fusion.119
  192.2 0.5 multiply_add_fusion.120
  194.3 0.5 multiply_add_fusion.122
  195.3 31.5 %all-gather.8 = f32[8,70,256]{2,1,0:T(8,128)S(1)} all-gather(f32[1,70,256]{2,1,0:T(8,128)S(1)} %fusion.1023), channel_id=5, replica_groups=mesh['tm'=8,'env'=4] {'tm'}, dimensions={0}, use_global_device_ids=true | all-gather | bytes 645120 | tf_op jit(solution)/shard_map/all_gather | solution.py:113
  226.9 0.7 fusion.1022
  228.0 17.2 %while.93 = (s32[]{:T(128)}, f32[2,35,256]{2,1,0:T(8,128)S(1)}, f32[2,35,256]{2,1,0:T(8,128)S(1)}, f32[35]{0:T(128)S(1)}, f32[2,35,256]{2,1,0:T(8,128)S(1)}, /*i...) while((s32[]{:T(128)}, f32[2,35,256]{2,1,0:T(8,128)S(1)}, ...), condition=%wide.region_13.14_spmd, body=%wide.region_12.13_spmd.sunk | while | flops 62504960 | bytes 2680981 | solution.py:52
  245.1 17.2 %while.94 = (s32[]{:T(128)}, f32[2,35,256]{2,1,0:T(8,128)S(1)}, f32[2,35,256]{2,1,0:T(8,128)S(1)}, f32[35]{0:T(128)S(1)}, f32[2,35,256]{2,1,0:T(8,128)S(1)}, /*i...) while((s32[]{:T(128)}, f32[2,35,256]{2,1,0:T(8,128)S(1)}, ...), condition=%wide.region_15.16_spmd, body=%wide.region_14.15_spmd.sunk | while | flops 62504960 | bytes 2680981 | solution.py:52
  245.7 0.5 multiply_add_fusion.127
  248.9 0.5 multiply_add_fusion.130
  250.0 0.5 multiply_add_fusion.127
  253.2 0.5 multiply_add_fusion.130
  254.3 0.5 multiply_add_fusion.127
  257.5 0.5 multiply_add_fusion.130
  258.6 0.5 multiply_add_fusion.127
  261.8 0.5 multiply_add_fusion.130
  262.8 31.3 %all-gather.9 = f32[8,70,256]{2,1,0:T(8,128)S(1)} all-gather(f32[1,70,256]{2,1,0:T(8,128)S(1)} %fusion.1021), channel_id=6, replica_groups=mesh['tm'=8,'env'=4] {'tm'}, dimensions={0}, use_global_device_ids=true | all-gather | bytes 645120 | tf_op jit(solution)/shard_map/all_gather | solution.py:113
  294.2 0.7 fusion.1020
  295.3 0.7 copy.115
  296.1 21.2 %all-reduce = (f32[1,256]{1,0:T(1,128)S(1)}, f32[1,256]{1,0:T(1,128)S(1)}, f32[1,256]{1,0:T(1,128)S(1)}) all-reduce(f32[1,256]{1,0:T(1,128)S(1)} %bitcast.663, f32[1,256]{1,0:T(1,128)S(1)} %bitcast.664, f32[1,256]{1,0:T(1,128)S(1)} %bitcast.662), channel_id=1, replica_groups=mesh['tm'=8,'env'=4] {'tm'}, use_global_device_ids=true, to_apply=%region_24.25 | all-reduce | flops 768 | bytes 6144 | tf_op jit(solution)/shard_map/pmax | solution.py:135
  317.3 0.6 pad_maximum_fusion.14
  (254 shorter events, 93.9 us)
Async XLA Ops:
  0.6 56.9 %copy-start = (f32[70,256]{1,0:T(8,128)S(1)}, f32[70,256]{1,0:T(8,128)}, u32[]{:S(2)}) copy-start(f32[70,256]{1,0:T(8,128)} %param.23) | copy-start | bytes 215044
  10.2 0.7 copy-start.4
  10.2 0.7 copy-start.5
  10.8 0.7 copy-start.1
  10.8 0.7 copy-start.2
  10.8 0.7 copy-start.3
  11.8 0.8 copy-start.6
  57.6 0.9 copy-start.7
  92.3 0.7 copy-start.8
where the time goes:
time: 318 us
  blocking collectives  187 us (59%)
  matrix products  111 us (35%)
  local copies, waits for them, and re-layouts  9.75 us (3%)
  loops' own time  7.26 us (2%)
    all_gather x4, blocking collectives, sweep(): lax.all_gather(local_shift[None], 'tm', axis=0, tiled=True)  126 us
    dot_general x220, matrix products, exact_dot(): jnp.dot(left, right, precision=lax.Precision.HIGHEST, preferred_element_t...  108 us
    all_gather x1, blocking collectives, body(): all_maps = lax.all_gather(device_map[None], 'tm', axis=0, tiled=True)  31.3 us
    pmax x1, blocking collectives, body(): records.append(lax.pmax(local_max, 'tm'))  21.2 us
    psum x1, blocking collectives, body(): totals = lax.psum(jnp.sum(contact_float, axis=1), 'env')  8.39 us

commit v1 on v0

--- a/solution.py
+++ b/solution.py
@@ -8,6 +8,18 @@
 SUB = 32
 ITERS = 3
 step_length = 0.05
+
+
+def product_in_turn(value, axis, dim, term):
+    size, index, span = (lax.axis_size(axis), lax.axis_index(axis), value.shape[dim])
+    forward = [(i, (i + 1) % size) for i in range(size)]
+    held, total = (value, None)
+    for step in range(size):
+        arriving = lax.ppermute(held, axis, forward) if step < size - 1 else None
+        update = term(held, (index - step) % size * span)
+        total = update if total is None else total + update
+        held = arriving
+    return total
 
 
 def exact_dot(left, right):
@@ -107,11 +119,16 @@
         local_shift = zero_shift
         for slot_pos in range(local_slices):
             local_shift = exact_dot(step_maps[slot_pos], local_shift) + offsets[slot_pos]
-        entry = lead_state + jnp.einsum(
-            "mij,mje->ie",
-            phi_rows,
-            lax.all_gather(local_shift[None], "tm", axis=0, tiled=True),
-            precision=lax.Precision.HIGHEST,
+        entry = lead_state + product_in_turn(
+            local_shift[None],
+            "tm",
+            0,
+            lambda shard, offset: jnp.einsum(
+                "mij,mje->ie",
+                lax.dynamic_slice_in_dim(phi_rows, offset, shard.shape[0], axis=0),
+                shard,
+                precision=lax.Precision.HIGHEST,
+            ),
         )
         start_list = []
         end_list = []

time: 318 us -> 381 us (1.20)
  waiting for transfers between devices: 0 us -> 184 us
  blocking collectives: 187 us -> 56.7 us
  matrix products: 111 us -> 117 us
    ppermute x0 -> x28, waiting for transfers between devices: none -> 184 us  [product_in_turn(): arriving = lax.ppermute(held, axis, forward) if step < size - 1 else None]
    all_gather x4 -> x0, blocking collectives: 126 us -> none  [sweep(): lax.all_gather(local_shift[None], 'tm', axis=0, tiled=True)]
    dot_general x4 -> x32, matrix products: 2.69 us -> 8.6 us  [sweep(): jnp.einsum('mij,mje->ie', lax.dynamic_slice_in_dim(phi_rows, offset, shar...]
    pmax x1, blocking collectives: 21.2 us -> 17.1 us  [body(): records.append(lax.pmax(local_max, 'tm'))]
  transfers between devices with their start and end apart: 0 -> 28, of which waited for: 0 -> 27; matrix products, arithmetic and copies ran while one was open for 0% -> 4% of each run, Pallas kernels for 0% -> 0%
where the time goes in v1:
time: 381 us; the launch traced here: 380 us
  waiting for transfers between devices  184 us (48%)
  matrix products  117 us (31%)
  blocking collectives  56.7 us (15%)
  local copies, waits for them, and re-layouts  9.48 us (2%)
  loops' own time  7.21 us (2%)
    ppermute x28, waiting for transfers between devices, product_in_turn(): arriving = lax.ppermute(held, axis, forward) if step < size - 1 else None  184 us
    dot_general x220, matrix products, exact_dot(): jnp.dot(left, right, precision=lax.Precision.HIGHEST, preferred_element_t...  108 us
    all_gather x1, blocking collectives, body(): all_maps = lax.all_gather(device_map[None], 'tm', axis=0, tiled=True)  31.1 us
    pmax x1, blocking collectives, body(): records.append(lax.pmax(local_max, 'tm'))  17.1 us
    dot_general x32, matrix products, sweep(): jnp.einsum('mij,mje->ie', lax.dynamic_slice_in_dim(phi_rows, offset, shar...  8.6 us
    psum x1, blocking collectives, body(): totals = lax.psum(jnp.sum(contact_float, axis=1), 'env')  8.4 us
  transfers between devices with their start and end apart: 28, of which 27 were waited for; matrix products, arithmetic and copies ran while one was open for 4% of the time, Pallas kernels for 0%

profile of v1, /device:TPU:0, one launch (start us, length us, event | category | flops | bytes accessed | tf_op | source)
XLA Modules:
  0.0 380.4 jit_solution(9937002521257712259)
XLA Ops:
  0.6 0.8 convert_reduce_fusion
  1.5 8.4 %psum.7 = f32[4]{0:T(128)S(1)} all-reduce(f32[4]{0:T(128)S(1)} %convert_reduce_fusion), channel_id=1, replica_groups=mesh['tm'=8,'env'=4] {'env'}, use_global_device_ids=true, to_apply=%region_1.0 | all-reduce | flops 4 | bytes 32 | tf_op jit(solution)/shard_map/psum | solution.py:86
  10.4 0.6 copy-done.4
  11.0 0.6 copy-done.1
  14.5 1.5 collective-permute-start
  16.2 0.7 copy-done.8
  17.1 31.1 %all-gather.1 = f32[8,70,70]{2,1,0:T(8,128)S(1)} all-gather(f32[1,70,70]{2,1,0:T(8,128)S(1)} %convolution_bitcast_fusion.1), channel_id=2, replica_groups=mesh['tm'=8,'env'=4] {'tm'}, dimensions={0}, use_global_device_ids=true | all-gather | bytes 176400 | tf_op jit(solution)/shard_map/all_gather | solution.py:104
  48.3 12.9 %while.95 = (s32[]{:T(128)}, f32[70,70]{0,1:T(8,128)S(1)}, f32[8,70,70]{1,2,0:T(8,128)S(1)}, s32[8]{0:T(128)S(1)}, s32[]{:T(128)}, /*index=5*/f32[8,70,70]{2,1,0:T(8,128)S(1)}, s32[]{:T(128)}, s32[]{:T(128)}) while((s32[]{:T(128)}, f32[70,70]{0,1:T(8,128)S(1)}, f32[8,70,70]{1,2,0:T(8,128)S(1)}, s32[8]{0:T(128)S(1)}, s32[]{:T(128)}, ...), condition=%wide.region_3.4_spmd.clone, body=%wide.region_2.3_spmd.clone.sunk | while | flops 4135604 | bytes 206392 | solution.py:115
  48.3 0.7 dynamic_slice.213
  49.9 0.7 dynamic_slice.213
  51.5 0.7 dynamic_slice.213
  53.1 0.7 dynamic_slice.213
  54.7 0.7 dynamic_slice.213
  56.3 0.7 dynamic_slice.213
  57.9 0.7 dynamic_slice.213
  59.5 0.7 dynamic_slice.213
  62.0 0.6 collective-permute-start.1
  62.9 6.2 %collective-permute-done.1 = f32[1,70,256]{2,1,0:T(8,128)S(1)} collective-permute-done((f32[1,70,256]{2,1,0:T(8,128)S(1)}, f32[1,70,256]{2,1,0:T(8,128)S(1)}, u32[]{:S(2)}, u32[]{:S(2)}) %collective-permute-start.1) | collective-permute-done | bytes 71712 | tf_op jit(solution)/shard_map/ppermute | solution.py:18
  69.4 6.8 %collective-permute-done.2 = f32[1,70,256]{2,1,0:T(8,128)S(1)} collective-permute-done((f32[1,70,256]{2,1,0:T(8,128)S(1)}, f32[1,70,256]{2,1,0:T(8,128)S(1)}, u32[]{:S(2)}, u32[]{:S(2)}) %collective-permute-start.2) | collective-permute-done | bytes 71712 | tf_op jit(solution)/shard_map/ppermute | solution.py:18
  76.4 6.8 %collective-permute-done.3 = f32[1,70,256]{2,1,0:T(8,128)S(1)} collective-permute-done((f32[1,70,256]{2,1,0:T(8,128)S(1)}, f32[1,70,256]{2,1,0:T(8,128)S(1)}, u32[]{:S(2)}, u32[]{:S(2)}) %collective-permute-start.3) | collective-permute-done | bytes 71712 | tf_op jit(solution)/shard_map/ppermute | solution.py:18
  83.5 7.5 %collective-permute-done.4 = f32[1,70,256]{2,1,0:T(8,128)S(1)} collective-permute-done((f32[1,70,256]{2,1,0:T(8,128)S(1)}, f32[1,70,256]{2,1,0:T(8,128)S(1)}, u32[]{:S(2)}, u32[]{:S(2)}) %collective-permute-start.4) | collective-permute-done | bytes 71712 | tf_op jit(solution)/shard_map/ppermute | solution.py:18
  91.3 6.8 %collective-permute-done.5 = f32[1,70,256]{2,1,0:T(8,128)S(1)} collective-permute-done((f32[1,70,256]{2,1,0:T(8,128)S(1)}, f32[1,70,256]{2,1,0:T(8,128)S(1)}, u32[]{:S(2)}, u32[]{:S(2)}) %collective-permute-start.5) | collective-permute-done | bytes 71712 | tf_op jit(solution)/shard_map/ppermute | solution.py:18
  98.3 6.8 %collective-permute-done.6 = f32[1,70,256]{2,1,0:T(8,128)S(1)} collective-permute-done((f32[1,70,256]{2,1,0:T(8,128)S(1)}, f32[1,70,256]{2,1,0:T(8,128)S(1)}, u32[]{:S(2)}, u32[]{:S(2)}) %collective-permute-start.6) | collective-permute-done | bytes 71712 | tf_op jit(solution)/shard_map/ppermute | solution.py:18
  105.6 17.2 %while.89 = (s32[]{:T(128)}, f32[2,35,256]{2,1,0:T(8,128)S(1)}, f32[2,35,256]{2,1,0:T(8,128)S(1)}, f32[35]{0:T(128)S(1)}, f32[2,35,256]{2,1,0:T(8,128)S(1)}, /*i...) while((s32[]{:T(128)}, f32[2,35,256]{2,1,0:T(8,128)S(1)}, ...), condition=%wide.region_5.6_spmd, body=%wide.region_4.5_spmd.sunk | while | flops 62504960 | bytes 2680981 | solution.py:64
  106.1 0.5 multiply_add_fusion.107
  107.2 0.5 multiply_add_fusion.108
  110.4 0.5 multiply_add_fusion.107
  111.5 0.5 multiply_add_fusion.108
  119.0 0.5 multiply_add_fusion.107
  120.1 0.5 multiply_add_fusion.108
  122.8 17.2 %while.90 = (s32[]{:T(128)}, f32[2,35,256]{2,1,0:T(8,128)S(1)}, f32[2,35,256]{2,1,0:T(8,128)S(1)}, f32[35]{0:T(128)S(1)}, f32[2,35,256]{2,1,0:T(8,128)S(1)}, /*i...) while((s32[]{:T(128)}, f32[2,35,256]{2,1,0:T(8,128)S(1)}, ...), condition=%wide.region_7.8_spmd, body=%wide.region_6.7_spmd.sunk | while | flops 62504960 | bytes 2680981 | solution.py:64
  141.0 6.8 %collective-permute-done.7 = f32[1,70,256]{2,1,0:T(8,128)S(1)} collective-permute-done((f32[1,70,256]{2,1,0:T(8,128)S(1)}, f32[1,70,256]{2,1,0:T(8,128)S(1)}, u32[]{:S(2)}, u32[]{:S(2)}) %collective-permute-start.7) | collective-permute-done | bytes 71712 | tf_op jit(solution)/shard_map/ppermute | solution.py:18
  148.1 6.8 %collective-permute-done.8 = f32[1,70,256]{2,1,0:T(8,128)S(1)} collective-permute-done((f32[1,70,256]{2,1,0:T(8,128)S(1)}, f32[1,70,256]{2,1,0:T(8,128)S(1)}, u32[]{:S(2)}, u32[]{:S(2)}) %collective-permute-start.8) | collective-permute-done | bytes 71712 | tf_op jit(solution)/shard_map/ppermute | solution.py:18
  155.1 7.2 %collective-permute-done.9 = f32[1,70,256]{2,1,0:T(8,128)S(1)} collective-permute-done((f32[1,70,256]{2,1,0:T(8,128)S(1)}, f32[1,70,256]{2,1,0:T(8,128)S(1)}, u32[]{:S(2)}, u32[]{:S(2)}) %collective-permute-start.9) | collective-permute-done | bytes 71712 | tf_op jit(solution)/shard_map/ppermute | solution.py:18
  162.6 6.8 %collective-permute-done.10 = f32[1,70,256]{2,1,0:T(8,128)S(1)} collective-permute-done((f32[1,70,256]{2,1,0:T(8,128)S(1)}, f32[1,70,256]{2,1,0:T(8,128)S(1)}, u32[]{:S(2)}, u32[]{:S(2)}) %collective-permute-start.10) | collective-permute-done | bytes 71712 | tf_op jit(solution)/shard_map/ppermute | solution.py:18
  169.7 6.8 %collective-permute-done.11 = f32[1,70,256]{2,1,0:T(8,128)S(1)} collective-permute-done((f32[1,70,256]{2,1,0:T(8,128)S(1)}, f32[1,70,256]{2,1,0:T(8,128)S(1)}, u32[]{:S(2)}, u32[]{:S(2)}) %collective-permute-start.11) | collective-permute-done | bytes 71712 | tf_op jit(solution)/shard_map/ppermute | solution.py:18
  176.7 6.8 %collective-permute-done.12 = f32[1,70,256]{2,1,0:T(8,128)S(1)} collective-permute-done((f32[1,70,256]{2,1,0:T(8,128)S(1)}, f32[1,70,256]{2,1,0:T(8,128)S(1)}, u32[]{:S(2)}, u32[]{:S(2)}) %collective-permute-start.12) | collective-permute-done | bytes 71712 | tf_op jit(solution)/shard_map/ppermute | solution.py:18
  183.8 6.8 %collective-permute-done.13 = f32[1,70,256]{2,1,0:T(8,128)S(1)} collective-permute-done((f32[1,70,256]{2,1,0:T(8,128)S(1)}, f32[1,70,256]{2,1,0:T(8,128)S(1)}, u32[]{:S(2)}, u32[]{:S(2)}) %collective-permute-start.13) | collective-permute-done | bytes 71712 | tf_op jit(solution)/shard_map/ppermute | solution.py:18
  191.1 17.2 %while.91 = (s32[]{:T(128)}, f32[2,35,256]{2,1,0:T(8,128)S(1)}, f32[2,35,256]{2,1,0:T(8,128)S(1)}, f32[35]{0:T(128)S(1)}, f32[2,35,256]{2,1,0:T(8,128)S(1)}, /*i...) while((s32[]{:T(128)}, f32[2,35,256]{2,1,0:T(8,128)S(1)}, ...), condition=%wide.region_9.10_spmd, body=%wide.region_8.9_spmd.sunk | while | flops 62504960 | bytes 2680981 | solution.py:64
  191.6 0.5 multiply_add_fusion.115
  192.7 0.5 multiply_add_fusion.116
  204.5 0.5 multiply_add_fusion.115
  205.5 0.5 multiply_add_fusion.116
  208.2 17.2 %while.92 = (s32[]{:T(128)}, f32[2,35,256]{2,1,0:T(8,128)S(1)}, f32[2,35,256]{2,1,0:T(8,128)S(1)}, f32[35]{0:T(128)S(1)}, f32[2,35,256]{2,1,0:T(8,128)S(1)}, /*i...) while((s32[]{:T(128)}, f32[2,35,256]{2,1,0:T(8,128)S(1)}, ...), condition=%wide.region_11.12_spmd, body=%wide.region_10.11_spmd.sunk | while | flops 62504960 | bytes 2680981 | solution.py:64
  226.4 6.8 %collective-permute-done.14 = f32[1,70,256]{2,1,0:T(8,128)S(1)} collective-permute-done((f32[1,70,256]{2,1,0:T(8,128)S(1)}, f32[1,70,256]{2,1,0:T(8,128)S(1)}, u32[]{:S(2)}, u32[]{:S(2)}) %collective-permute-start.14) | collective-permute-done | bytes 71712 | tf_op jit(solution)/shard_map/ppermute | solution.py:18
  233.6 7.2 %collective-permute-done.15 = f32[1,70,256]{2,1,0:T(8,128)S(1)} collective-permute-done((f32[1,70,256]{2,1,0:T(8,128)S(1)}, f32[1,70,256]{2,1,0:T(8,128)S(1)}, u32[]{:S(2)}, u32[]{:S(2)}) %collective-permute-start.15) | collective-permute-done | bytes 71712 | tf_op jit(solution)/shard_map/ppermute | solution.py:18
  241.1 6.8 %collective-permute-done.16 = f32[1,70,256]{2,1,0:T(8,128)S(1)} collective-permute-done((f32[1,70,256]{2,1,0:T(8,128)S(1)}, f32[1,70,256]{2,1,0:T(8,128)S(1)}, u32[]{:S(2)}, u32[]{:S(2)}) %collective-permute-start.16) | collective-permute-done | bytes 71712 | tf_op jit(solution)/shard_map/ppermute | solution.py:18
  248.1 6.8 %collective-permute-done.17 = f32[1,70,256]{2,1,0:T(8,128)S(1)} collective-permute-done((f32[1,70,256]{2,1,0:T(8,128)S(1)}, f32[1,70,256]{2,1,0:T(8,128)S(1)}, u32[]{:S(2)}, u32[]{:S(2)}) %collective-permute-start.17) | collective-permute-done | bytes 71712 | tf_op jit(solution)/shard_map/ppermute | solution.py:18
  255.2 6.8 %collective-permute-done.18 = f32[1,70,256]{2,1,0:T(8,128)S(1)} collective-permute-done((f32[1,70,256]{2,1,0:T(8,128)S(1)}, f32[1,70,256]{2,1,0:T(8,128)S(1)}, u32[]{:S(2)}, u32[]{:S(2)}) %collective-permute-start.18) | collective-permute-done | bytes 71712 | tf_op jit(solution)/shard_map/ppermute | solution.py:18
  262.2 6.8 %collective-permute-done.19 = f32[1,70,256]{2,1,0:T(8,128)S(1)} collective-permute-done((f32[1,70,256]{2,1,0:T(8,128)S(1)}, f32[1,70,256]{2,1,0:T(8,128)S(1)}, u32[]{:S(2)}, u32[]{:S(2)}) %collective-permute-start.19) | collective-permute-done | bytes 71712 | tf_op jit(solution)/shard_map/ppermute | solution.py:18
  269.3 6.8 %collective-permute-done.20 = f32[1,70,256]{2,1,0:T(8,128)S(1)} collective-permute-done((f32[1,70,256]{2,1,0:T(8,128)S(1)}, f32[1,70,256]{2,1,0:T(8,128)S(1)}, u32[]{:S(2)}, u32[]{:S(2)}) %collective-permute-start.20) | collective-permute-done | bytes 71712 | tf_op jit(solution)/shard_map/ppermute | solution.py:18
  276.5 17.2 %while.93 = (s32[]{:T(128)}, f32[2,35,256]{2,1,0:T(8,128)S(1)}, f32[2,35,256]{2,1,0:T(8,128)S(1)}, f32[35]{0:T(128)S(1)}, f32[2,35,256]{2,1,0:T(8,128)S(1)}, /*i...) while((s32[]{:T(128)}, f32[2,35,256]{2,1,0:T(8,128)S(1)}, ...), condition=%wide.region_13.14_spmd, body=%wide.region_12.13_spmd.sunk | while | flops 62504960 | bytes 2680981 | solution.py:64
  282.4 0.5 multiply_add_fusion.124
  293.7 17.1 %while.94 = (s32[]{:T(128)}, f32[2,35,256]{2,1,0:T(8,128)S(1)}, f32[2,35,256]{2,1,0:T(8,128)S(1)}, f32[35]{0:T(128)S(1)}, f32[2,35,256]{2,1,0:T(8,128)S(1)}, /*i...) while((s32[]{:T(128)}, f32[2,35,256]{2,1,0:T(8,128)S(1)}, ...), condition=%wide.region_15.16_spmd, body=%wide.region_14.15_spmd.sunk | while | flops 62504960 | bytes 2680981 | solution.py:64
  311.9 6.8 %collective-permute-done.21 = f32[1,70,256]{2,1,0:T(8,128)S(1)} collective-permute-done((f32[1,70,256]{2,1,0:T(8,128)S(1)}, f32[1,70,256]{2,1,0:T(8,128)S(1)}, u32[]{:S(2)}, u32[]{:S(2)}) %collective-permute-start.21) | collective-permute-done | bytes 71712 | tf_op jit(solution)/shard_map/ppermute | solution.py:18
  319.0 6.8 %collective-permute-done.22 = f32[1,70,256]{2,1,0:T(8,128)S(1)} collective-permute-done((f32[1,70,256]{2,1,0:T(8,128)S(1)}, f32[1,70,256]{2,1,0:T(8,128)S(1)}, u32[]{:S(2)}, u32[]{:S(2)}) %collective-permute-start.22) | collective-permute-done | bytes 71712 | tf_op jit(solution)/shard_map/ppermute | solution.py:18
  326.1 6.8 %collective-permute-done.23 = f32[1,70,256]{2,1,0:T(8,128)S(1)} collective-permute-done((f32[1,70,256]{2,1,0:T(8,128)S(1)}, f32[1,70,256]{2,1,0:T(8,128)S(1)}, u32[]{:S(2)}, u32[]{:S(2)}) %collective-permute-start.23) | collective-permute-done | bytes 71712 | tf_op jit(solution)/shard_map/ppermute | solution.py:18
  333.2 6.8 %collective-permute-done.24 = f32[1,70,256]{2,1,0:T(8,128)S(1)} collective-permute-done((f32[1,70,256]{2,1,0:T(8,128)S(1)}, f32[1,70,256]{2,1,0:T(8,128)S(1)}, u32[]{:S(2)}, u32[]{:S(2)}) %collective-permute-start.24) | collective-permute-done | bytes 71712 | tf_op jit(solution)/shard_map/ppermute | solution.py:18
  340.2 6.8 %collective-permute-done.25 = f32[1,70,256]{2,1,0:T(8,128)S(1)} collective-permute-done((f32[1,70,256]{2,1,0:T(8,128)S(1)}, f32[1,70,256]{2,1,0:T(8,128)S(1)}, u32[]{:S(2)}, u32[]{:S(2)}) %collective-permute-start.25) | collective-permute-done | bytes 71712 | tf_op jit(solution)/shard_map/ppermute | solution.py:18
  347.3 6.8 %collective-permute-done.26 = f32[1,70,256]{2,1,0:T(8,128)S(1)} collective-permute-done((f32[1,70,256]{2,1,0:T(8,128)S(1)}, f32[1,70,256]{2,1,0:T(8,128)S(1)}, u32[]{:S(2)}, u32[]{:S(2)}) %collective-permute-start.26) | collective-permute-done | bytes 71712 | tf_op jit(solution)/shard_map/ppermute | solution.py:18
  354.3 6.8 %collective-permute-done.27 = f32[1,70,256]{2,1,0:T(8,128)S(1)} collective-permute-done((f32[1,70,256]{2,1,0:T(8,128)S(1)}, f32[1,70,256]{2,1,0:T(8,128)S(1)}, u32[]{:S(2)}, u32[]{:S(2)}) %collective-permute-start.27) | collective-permute-done | bytes 71712 | tf_op jit(solution)/shard_map/ppermute | solution.py:18
  361.9 0.7 copy.101
  362.7 17.1 %all-reduce = (f32[1,256]{1,0:T(1,128)S(1)}, f32[1,256]{1,0:T(1,128)S(1)}, f32[1,256]{1,0:T(1,128)S(1)}) all-reduce(f32[1,256]{1,0:T(1,128)S(1)} %bitcast.799, f32[1,256]{1,0:T(1,128)S(1)} %bitcast.800, f32[1,256]{1,0:T(1,128)S(1)} %bitcast.798), channel_id=1, replica_groups=mesh['tm'=8,'env'=4] {'tm'}, use_global_device_ids=true, to_apply=%region_24.25 | all-reduce | flops 768 | bytes 6144 | tf_op jit(solution)/shard_map/pmax | solution.py:152
  379.8 0.6 pad_maximum_fusion.14
  (334 shorter events, 113.6 us)
Async XLA Ops:
  0.6 60.5 %copy-start = (f32[70,256]{1,0:T(8,128)S(1)}, f32[70,256]{1,0:T(8,128)}, u32[]{:S(2)}) copy-start(f32[70,256]{1,0:T(8,128)} %param.23) | copy-start | bytes 215044
  10.3 0.7 copy-start.4
  10.3 0.7 copy-start.5
  10.3 1.4 copy-start.6
  11.0 0.7 copy-start.1
  11.0 0.7 copy-start.2
  11.0 0.7 copy-start.3
  12.4 0.9 copy-start.7
  14.5 47.5 %collective-permute-start = (f32[1,70,256]{2,1,0:T(8,128)S(1)}, f32[1,70,256]{2,1,0:T(8,128)S(1)}, u32[]{:S(2)}, u32[]{:S(2)}) collective-permute-start(f32[1,70,256]{2,1,0:T(8,128)S(1)} %bitcast.793), channel_id=1, source_target_pairs={{0,4},{4,8},{8,12},{12,16},{16,20},{20,24},{24,28},{28,0},{1,5},{5... | collective-permute-start | bytes 215048 | tf_op jit(solution)/shard_map/ppermute | solution.py:18
  16.2 0.7 copy-start.8
  62.0 7.1 %collective-permute-start.1 = (f32[1,70,256]{2,1,0:T(8,128)S(1)}, f32[1,70,256]{2,1,0:T(8,128)S(1)}, u32[]{:S(2)}, u32[]{:S(2)}) collective-permute-start(f32[1,70,256]{2,1,0:T(8,128)S(1)} %collective-permute-done), channel_id=1, source_target_pairs={{0,4},{4,8},{8,12},{12,16},{16,20},{20,24},{24,28},{28,0},{1,5},{5... | collective-permute-start | bytes 215048 | tf_op jit(solution)/shard_map/ppermute | solution.py:18
  69.1 7.0 %collective-permute-start.2 = (f32[1,70,256]{2,1,0:T(8,128)S(1)}, f32[1,70,256]{2,1,0:T(8,128)S(1)}, u32[]{:S(2)}, u32[]{:S(2)}) collective-permute-start(f32[1,70,256]{2,1,0:T(8,128)S(1)} %collective-permute-done.1), channel_id=1, source_target_pairs={{0,4},{4,8},{8,12},{12,16},{16,20},{20,24},{24,28},{28,0},{1,5},{5... | collective-permute-start | bytes 215048 | tf_op jit(solution)/shard_map/ppermute | solution.py:18
  76.2 7.0 %collective-permute-start.3 = (f32[1,70,256]{2,1,0:T(8,128)S(1)}, f32[1,70,256]{2,1,0:T(8,128)S(1)}, u32[]{:S(2)}, u32[]{:S(2)}) collective-permute-start(f32[1,70,256]{2,1,0:T(8,128)S(1)} %collective-permute-done.2), channel_id=1, source_target_pairs={{0,4},{4,8},{8,12},{12,16},{16,20},{20,24},{24,28},{28,0},{1,5},{5... | collective-permute-start | bytes 215048 | tf_op jit(solution)/shard_map/ppermute | solution.py:18
  83.2 7.8 %collective-permute-start.4 = (f32[1,70,256]{2,1,0:T(8,128)S(1)}, f32[1,70,256]{2,1,0:T(8,128)S(1)}, u32[]{:S(2)}, u32[]{:S(2)}) collective-permute-start(f32[1,70,256]{2,1,0:T(8,128)S(1)} %collective-permute-done.3), channel_id=1, source_target_pairs={{0,4},{4,8},{8,12},{12,16},{16,20},{20,24},{24,28},{28,0},{1,5},{5... | collective-permute-start | bytes 215048 | tf_op jit(solution)/shard_map/ppermute | solution.py:18
  91.0 7.0 %collective-permute-start.5 = (f32[1,70,256]{2,1,0:T(8,128)S(1)}, f32[1,70,256]{2,1,0:T(8,128)S(1)}, u32[]{:S(2)}, u32[]{:S(2)}) collective-permute-start(f32[1,70,256]{2,1,0:T(8,128)S(1)} %collective-permute-done.4), channel_id=1, source_target_pairs={{0,4},{4,8},{8,12},{12,16},{16,20},{20,24},{24,28},{28,0},{1,5},{5... | collective-permute-start | bytes 215048 | tf_op jit(solution)/shard_map/ppermute | solution.py:18
  98.0 7.1 %collective-permute-start.6 = (f32[1,70,256]{2,1,0:T(8,128)S(1)}, f32[1,70,256]{2,1,0:T(8,128)S(1)}, u32[]{:S(2)}, u32[]{:S(2)}) collective-permute-start(f32[1,70,256]{2,1,0:T(8,128)S(1)} %collective-permute-done.5), channel_id=1, source_target_pairs={{0,4},{4,8},{8,12},{12,16},{16,20},{20,24},{24,28},{28,0},{1,5},{5... | collective-permute-start | bytes 215048 | tf_op jit(solution)/shard_map/ppermute | solution.py:18
  140.7 7.1 %collective-permute-start.7 = (f32[1,70,256]{2,1,0:T(8,128)S(1)}, f32[1,70,256]{2,1,0:T(8,128)S(1)}, u32[]{:S(2)}, u32[]{:S(2)}) collective-permute-start(f32[1,70,256]{2,1,0:T(8,128)S(1)} %bitcast.795), channel_id=1, source_target_pairs={{0,4},{4,8},{8,12},{12,16},{16,20},{20,24},{24,28},{28,0},{1,5},{5... | collective-permute-start | bytes 215048 | tf_op jit(solution)/shard_map/ppermute | solution.py:18
  147.8 7.0 %collective-permute-start.8 = (f32[1,70,256]{2,1,0:T(8,128)S(1)}, f32[1,70,256]{2,1,0:T(8,128)S(1)}, u32[]{:S(2)}, u32[]{:S(2)}) collective-permute-start(f32[1,70,256]{2,1,0:T(8,128)S(1)} %collective-permute-done.7), channel_id=1, source_target_pairs={{0,4},{4,8},{8,12},{12,16},{16,20},{20,24},{24,28},{28,0},{1,5},{5... | collective-permute-start | bytes 215048 | tf_op jit(solution)/shard_map/ppermute | solution.py:18
  154.9 7.5 %collective-permute-start.9 = (f32[1,70,256]{2,1,0:T(8,128)S(1)}, f32[1,70,256]{2,1,0:T(8,128)S(1)}, u32[]{:S(2)}, u32[]{:S(2)}) collective-permute-start(f32[1,70,256]{2,1,0:T(8,128)S(1)} %collective-permute-done.8), channel_id=1, source_target_pairs={{0,4},{4,8},{8,12},{12,16},{16,20},{20,24},{24,28},{28,0},{1,5},{5... | collective-permute-start | bytes 215048 | tf_op jit(solution)/shard_map/ppermute | solution.py:18
  162.3 7.1 %collective-permute-start.10 = (f32[1,70,256]{2,1,0:T(8,128)S(1)}, f32[1,70,256]{2,1,0:T(8,128)S(1)}, u32[]{:S(2)}, u32[]{:S(2)}) collective-permute-start(f32[1,70,256]{2,1,0:T(8,128)S(1)} %collective-permute-done.9), channel_id=1, source_target_pairs={{0,4},{4,8},{8,12},{12,16},{16,20},{20,24},{24,28},{28,0},{1,5},{5... | collective-permute-start | bytes 215048 | tf_op jit(solution)/shard_map/ppermute | solution.py:18
  169.4 7.0 %collective-permute-start.11 = (f32[1,70,256]{2,1,0:T(8,128)S(1)}, f32[1,70,256]{2,1,0:T(8,128)S(1)}, u32[]{:S(2)}, u32[]{:S(2)}) collective-permute-start(f32[1,70,256]{2,1,0:T(8,128)S(1)} %collective-permute-done.10), channel_id=1, source_target_pairs={{0,4},{4,8},{8,12},{12,16},{16,20},{20,24},{24,28},{28,0},{1,5},{5... | collective-permute-start | bytes 215048 | tf_op jit(solution)/shard_map/ppermute | solution.py:18
  176.4 7.0 %collective-permute-start.12 = (f32[1,70,256]{2,1,0:T(8,128)S(1)}, f32[1,70,256]{2,1,0:T(8,128)S(1)}, u32[]{:S(2)}, u32[]{:S(2)}) collective-permute-start(f32[1,70,256]{2,1,0:T(8,128)S(1)} %collective-permute-done.11), channel_id=1, source_target_pairs={{0,4},{4,8},{8,12},{12,16},{16,20},{20,24},{24,28},{28,0},{1,5},{5... | collective-permute-start | bytes 215048 | tf_op jit(solution)/shard_map/ppermute | solution.py:18
  183.5 7.1 %collective-permute-start.13 = (f32[1,70,256]{2,1,0:T(8,128)S(1)}, f32[1,70,256]{2,1,0:T(8,128)S(1)}, u32[]{:S(2)}, u32[]{:S(2)}) collective-permute-start(f32[1,70,256]{2,1,0:T(8,128)S(1)} %collective-permute-done.12), channel_id=1, source_target_pairs={{0,4},{4,8},{8,12},{12,16},{16,20},{20,24},{24,28},{28,0},{1,5},{5... | collective-permute-start | bytes 215048 | tf_op jit(solution)/shard_map/ppermute | solution.py:18
  226.2 7.1 %collective-permute-start.14 = (f32[1,70,256]{2,1,0:T(8,128)S(1)}, f32[1,70,256]{2,1,0:T(8,128)S(1)}, u32[]{:S(2)}, u32[]{:S(2)}) collective-permute-start(f32[1,70,256]{2,1,0:T(8,128)S(1)} %bitcast.796), channel_id=1, source_target_pairs={{0,4},{4,8},{8,12},{12,16},{16,20},{20,24},{24,28},{28,0},{1,5},{5... | collective-permute-start | bytes 215048 | tf_op jit(solution)/shard_map/ppermute | solution.py:18
  233.3 7.5 %collective-permute-start.15 = (f32[1,70,256]{2,1,0:T(8,128)S(1)}, f32[1,70,256]{2,1,0:T(8,128)S(1)}, u32[]{:S(2)}, u32[]{:S(2)}) collective-permute-start(f32[1,70,256]{2,1,0:T(8,128)S(1)} %collective-permute-done.14), channel_id=1, source_target_pairs={{0,4},{4,8},{8,12},{12,16},{16,20},{20,24},{24,28},{28,0},{1,5},{5... | collective-permute-start | bytes 215048 | tf_op jit(solution)/shard_map/ppermute | solution.py:18
  240.8 7.0 %collective-permute-start.16 = (f32[1,70,256]{2,1,0:T(8,128)S(1)}, f32[1,70,256]{2,1,0:T(8,128)S(1)}, u32[]{:S(2)}, u32[]{:S(2)}) collective-permute-start(f32[1,70,256]{2,1,0:T(8,128)S(1)} %collective-permute-done.15), channel_id=1, source_target_pairs={{0,4},{4,8},{8,12},{12,16},{16,20},{20,24},{24,28},{28,0},{1,5},{5... | collective-permute-start | bytes 215048 | tf_op jit(solution)/shard_map/ppermute | solution.py:18
  247.8 7.0 %collective-permute-start.17 = (f32[1,70,256]{2,1,0:T(8,128)S(1)}, f32[1,70,256]{2,1,0:T(8,128)S(1)}, u32[]{:S(2)}, u32[]{:S(2)}) collective-permute-start(f32[1,70,256]{2,1,0:T(8,128)S(1)} %collective-permute-done.16), channel_id=1, source_target_pairs={{0,4},{4,8},{8,12},{12,16},{16,20},{20,24},{24,28},{28,0},{1,5},{5... | collective-permute-start | bytes 215048 | tf_op jit(solution)/shard_map/ppermute | solution.py:18
  254.9 7.0 %collective-permute-start.18 = (f32[1,70,256]{2,1,0:T(8,128)S(1)}, f32[1,70,256]{2,1,0:T(8,128)S(1)}, u32[]{:S(2)}, u32[]{:S(2)}) collective-permute-start(f32[1,70,256]{2,1,0:T(8,128)S(1)} %collective-permute-done.17), channel_id=1, source_target_pairs={{0,4},{4,8},{8,12},{12,16},{16,20},{20,24},{24,28},{28,0},{1,5},{5... | collective-permute-start | bytes 215048 | tf_op jit(solution)/shard_map/ppermute | solution.py:18
  261.9 7.0 %collective-permute-start.19 = (f32[1,70,256]{2,1,0:T(8,128)S(1)}, f32[1,70,256]{2,1,0:T(8,128)S(1)}, u32[]{:S(2)}, u32[]{:S(2)}) collective-permute-start(f32[1,70,256]{2,1,0:T(8,128)S(1)} %collective-permute-done.18), channel_id=1, source_target_pairs={{0,4},{4,8},{8,12},{12,16},{16,20},{20,24},{24,28},{28,0},{1,5},{5... | collective-permute-start | bytes 215048 | tf_op jit(solution)/shard_map/ppermute | solution.py:18
  269.0 7.1 %collective-permute-start.20 = (f32[1,70,256]{2,1,0:T(8,128)S(1)}, f32[1,70,256]{2,1,0:T(8,128)S(1)}, u32[]{:S(2)}, u32[]{:S(2)}) collective-permute-start(f32[1,70,256]{2,1,0:T(8,128)S(1)} %collective-permute-done.19), channel_id=1, source_target_pairs={{0,4},{4,8},{8,12},{12,16},{16,20},{20,24},{24,28},{28,0},{1,5},{5... | collective-permute-start | bytes 215048 | tf_op jit(solution)/shard_map/ppermute | solution.py:18
  311.6 7.1 %collective-permute-start.21 = (f32[1,70,256]{2,1,0:T(8,128)S(1)}, f32[1,70,256]{2,1,0:T(8,128)S(1)}, u32[]{:S(2)}, u32[]{:S(2)}) collective-permute-start(f32[1,70,256]{2,1,0:T(8,128)S(1)} %bitcast.794), channel_id=1, source_target_pairs={{0,4},{4,8},{8,12},{12,16},{16,20},{20,24},{24,28},{28,0},{1,5},{5... | collective-permute-start | bytes 215048 | tf_op jit(solution)/shard_map/ppermute | solution.py:18
  318.8 7.0 %collective-permute-start.22 = (f32[1,70,256]{2,1,0:T(8,128)S(1)}, f32[1,70,256]{2,1,0:T(8,128)S(1)}, u32[]{:S(2)}, u32[]{:S(2)}) collective-permute-start(f32[1,70,256]{2,1,0:T(8,128)S(1)} %collective-permute-done.21), channel_id=1, source_target_pairs={{0,4},{4,8},{8,12},{12,16},{16,20},{20,24},{24,28},{28,0},{1,5},{5... | collective-permute-start | bytes 215048 | tf_op jit(solution)/shard_map/ppermute | solution.py:18
  325.8 7.1 %collective-permute-start.23 = (f32[1,70,256]{2,1,0:T(8,128)S(1)}, f32[1,70,256]{2,1,0:T(8,128)S(1)}, u32[]{:S(2)}, u32[]{:S(2)}) collective-permute-start(f32[1,70,256]{2,1,0:T(8,128)S(1)} %collective-permute-done.22), channel_id=1, source_target_pairs={{0,4},{4,8},{8,12},{12,16},{16,20},{20,24},{24,28},{28,0},{1,5},{5... | collective-permute-start | bytes 215048 | tf_op jit(solution)/shard_map/ppermute | solution.py:18
  332.9 7.0 %collective-permute-start.24 = (f32[1,70,256]{2,1,0:T(8,128)S(1)}, f32[1,70,256]{2,1,0:T(8,128)S(1)}, u32[]{:S(2)}, u32[]{:S(2)}) collective-permute-start(f32[1,70,256]{2,1,0:T(8,128)S(1)} %collective-permute-done.23), channel_id=1, source_target_pairs={{0,4},{4,8},{8,12},{12,16},{16,20},{20,24},{24,28},{28,0},{1,5},{5... | collective-permute-start | bytes 215048 | tf_op jit(solution)/shard_map/ppermute | solution.py:18
  339.9 7.0 %collective-permute-start.25 = (f32[1,70,256]{2,1,0:T(8,128)S(1)}, f32[1,70,256]{2,1,0:T(8,128)S(1)}, u32[]{:S(2)}, u32[]{:S(2)}) collective-permute-start(f32[1,70,256]{2,1,0:T(8,128)S(1)} %collective-permute-done.24), channel_id=1, source_target_pairs={{0,4},{4,8},{8,12},{12,16},{16,20},{20,24},{24,28},{28,0},{1,5},{5... | collective-permute-start | bytes 215048 | tf_op jit(solution)/shard_map/ppermute | solution.py:18
  347.0 7.0 %collective-permute-start.26 = (f32[1,70,256]{2,1,0:T(8,128)S(1)}, f32[1,70,256]{2,1,0:T(8,128)S(1)}, u32[]{:S(2)}, u32[]{:S(2)}) collective-permute-start(f32[1,70,256]{2,1,0:T(8,128)S(1)} %collective-permute-done.25), channel_id=1, source_target_pairs={{0,4},{4,8},{8,12},{12,16},{16,20},{20,24},{24,28},{28,0},{1,5},{5... | collective-permute-start | bytes 215048 | tf_op jit(solution)/shard_map/ppermute | solution.py:18
  354.1 7.0 %collective-permute-start.27 = (f32[1,70,256]{2,1,0:T(8,128)S(1)}, f32[1,70,256]{2,1,0:T(8,128)S(1)}, u32[]{:S(2)}, u32[]{:S(2)}) collective-permute-start(f32[1,70,256]{2,1,0:T(8,128)S(1)} %collective-permute-done.26), channel_id=1, source_target_pairs={{0,4},{4,8},{8,12},{12,16},{16,20},{20,24},{24,28},{28,0},{1,5},{5... | collective-permute-start | bytes 215048 | tf_op jit(solution)/shard_map/ppermute | solution.py:18
